TPU v7x, 128 devices: a whole 4x4x4 slice. The times are simulated.
128 devices in a mesh: section: 2 (over core), tp: 4 (over x), pool: 16 (over z, y).
Axes of the slice: x: 4, y: 4, z: 4, core: 2. Of those that a mesh axis runs over, the one named last changes fastest.
Arguments:
- hidden: bfloat16 [2, 16, 128, 8192], P('section', 'pool', None, 'tp'), may hold values from -6 to 6
- queries: bfloat16 [2, 16, 16, 8, 64, 128], P('section', 'pool', None, None, 'tp'), may hold values from -450 to 450, as said below
- window_key_value: bfloat16 [2, 16, 16, 2, 8, 8, 128], P('section', 'pool', None, None, 'tp'), may hold values from -12 to 12
- cached_key_value: bfloat16 [2, 16, 128, 2, 8, 64, 128], P('section', 'pool', None, None, 'tp'), may hold values from -12 to 12
- cached_length: int32 [2, 16, 16], P('section', 'pool'), may hold values from 1 to 1024, 6144 in all within a row
- request_page_table: int32 [2, 16, 16, 16], P('section', 'pool'), may hold values from 0 to 127
- request_adapter: int32 [2, 16, 16], replicated, may hold values from 0 to 127, as said below
- layer_page_slot: int32 [256], replicated, may hold values from 0 to 255, as said below
- wo: bfloat16 [2, 8192, 8192], P('section', 'tp'), may hold values from -0.09375 to 0.09375
- adapter_down: bfloat16 [256, 64, 8192], P(('section', 'pool'), None, 'tp'), may hold values from -0.0625 to 0.0625
- adapter_up: bfloat16 [256, 64, 8192], P(('section', 'pool'), None, 'tp'), may hold values from -0.75 to 0.75
Outputs:
- next_hidden: bfloat16 [2, 16, 128, 8192], P('section', 'pool', None, 'tp')
Inputs may be any that keep to these rules, and one draw needn't show every extreme that they name: `queries`: queries of order one; some entries far larger in the hidden draw. `request_page_table`: several requests may name the same cache page; entries past a request's length are read but excluded. `cached_length`: each request of a device has 1 to 1024 cached positions. `layer_page_slot`: the adapters of layer s occupy slots s * 128 to (s + 1) * 128 - 1, each slot once; slot q lies on the index q // 8 of section and pool taken together, section first, so layer s's pages sit on section s. `request_adapter`: up to all 16 requests of a pool group may use adapters held on one pool index, and one pool index may serve every request of its section.
All inputs are finite; a program needn't handle non-finite values.
Results may differ from a plain program's by a relative error of at most 0.009.
Values may be sent and summed in bfloat16 or wider, within the bound.
A program may use at most 192 MiB of HBM per device.

v0:
```python
import jax
import jax.numpy as jnp
from jax import lax
from jax.sharding import PartitionSpec as P


def from_behind(value, axis, steps):
    count = lax.axis_size(axis)
    pairs = [(source, (source + steps) % count) for source in range(count)]
    return lax.ppermute(value, axis, pairs)


def attend(queries, cache_pages, window_kv, lengths, page_rows):
    requests, window, head_count, head_size = queries.shape
    kv_heads = window_kv.shape[2]
    page_tok = cache_pages.shape[3]
    max_pages = page_rows.shape[1]
    cached = max_pages * page_tok
    picked = jnp.take(cache_pages, page_rows, axis=0)
    picked = jnp.transpose(picked, (0, 2, 3, 1, 4, 5)).reshape(
        requests, 2, kv_heads, cached, head_size
    )
    keys_all = jnp.concatenate([picked, window_kv], axis=3)
    grouped = queries.reshape(requests, window, kv_heads, head_count // kv_heads, head_size)
    scores = jnp.einsum(
        "rwkgd,rktd->rkgwt", grouped, keys_all[:, 0], preferred_element_type=jnp.float32
    ) * head_size ** (-0.5)
    position = jnp.arange(cached + window, dtype=jnp.int32)
    query_pos = jnp.arange(window, dtype=jnp.int32)
    in_cache = position[None, :] < lengths[:, None]
    in_window = (position[None, :] >= cached) & (position[None, :] - cached <= query_pos[:, None])
    allowed = in_cache[:, None, :] | in_window[None, :, :]
    scores = jnp.where(allowed[:, None, None, :, :], scores, -jnp.inf)
    largest = jnp.max(scores, axis=-1, keepdims=True)
    weights = jnp.exp(scores - largest)
    probs = (weights / jnp.sum(weights, axis=-1, keepdims=True)).astype(jnp.bfloat16)
    context = jnp.einsum(
        "rkgwt,rktd->rwkgd", probs, keys_all[:, 1], preferred_element_type=jnp.float32
    )
    return context.reshape(requests, window, head_count * head_size).astype(jnp.bfloat16)


def per_device(
    hidden,
    queries,
    window_key_value,
    cached_key_value,
    cached_length,
    request_page_table,
    request_adapter,
    layer_page_slot,
    wo,
    adapter_down,
    adapter_up,
):
    section_count = lax.axis_size("section")
    section_index = lax.axis_index("section")
    pool_index = lax.axis_index("pool")
    context = attend(
        queries[0, 0],
        cached_key_value[0, 0],
        window_key_value[0, 0],
        cached_length[0, 0],
        request_page_table[0, 0],
    )
    requests, window, width_of_head = context.shape
    flat_rows = context.reshape(requests * window, width_of_head)
    partial_out = jnp.dot(flat_rows, wo[0], preferred_element_type=jnp.float32)
    plain_output = lax.psum_scatter(partial_out, "tp", scatter_dimension=1, tiled=True)
    pages_per_member = adapter_down.shape[0]
    rank_width = adapter_down.shape[1]
    output_width = adapter_up.shape[2]
    adapters = layer_page_slot.shape[0] // section_count
    layer_start = section_index * adapters
    everyone = lax.all_gather(context, "pool", axis=0, tiled=True)
    total_requests = everyone.shape[0]
    all_slots = layer_page_slot[layer_start + request_adapter[section_index]].reshape(
        total_requests
    )
    local_slot = all_slots - layer_start - pool_index * pages_per_member
    owned_mask = (
        local_slot[:, None] == jnp.arange(pages_per_member, dtype=jnp.int32)[None, :]
    ).astype(jnp.float32)
    stacked_down = adapter_down.reshape(pages_per_member * rank_width, width_of_head)
    wide_rank = lax.dot_general(
        everyone, stacked_down, (((2,), (1,)), ((), ())), preferred_element_type=jnp.float32
    )
    wide_rank = wide_rank.reshape(total_requests, window, pages_per_member, rank_width)
    rank_hidden = jnp.sum(wide_rank * owned_mask[:, None, :, None], axis=2)
    rank_hidden = lax.psum(rank_hidden, "tp")
    broadcast_rows = (
        rank_hidden.astype(jnp.bfloat16)[:, :, None, :]
        * owned_mask.astype(jnp.bfloat16)[:, None, :, None]
    )
    broadcast_rows = broadcast_rows.reshape(total_requests * window, pages_per_member * rank_width)
    product = jnp.dot(
        broadcast_rows,
        adapter_up.reshape(pages_per_member * rank_width, output_width),
        preferred_element_type=jnp.float32,
    )
    returned = lax.all_to_all(
        product.astype(jnp.bfloat16), "pool", split_axis=0, concat_axis=0, tiled=True
    )
    adapter_delta = jnp.sum(
        returned.reshape(-1, requests * window, output_width).astype(jnp.float32), axis=0
    )
    blended_output = (hidden[0, 0].astype(jnp.float32) + plain_output + adapter_delta).astype(
        jnp.bfloat16
    )
    handed = from_behind(blended_output, "section", 1)
    return handed[None, None]


def solution(mesh):
    return jax.shard_map(
        per_device,
        mesh=mesh,
        in_specs=(
            P("section", "pool", None, "tp"),
            P("section", "pool", None, None, "tp", None),
            P("section", "pool", None, None, "tp", None, None),
            P("section", "pool", None, None, "tp", None, None),
            P("section", "pool", None),
            P("section", "pool", None, None),
            P(),
            P(),
            P("section", "tp", None),
            P(("section", "pool"), None, "tp"),
            P(("section", "pool"), None, "tp"),
        ),
        out_specs=P("section", "pool", None, "tp"),
        check_vma=False,
    )
```

profile of v0, /device:TPU:35, one launch (start us, length us, event | category | flops | bytes accessed | tf_op | source)
XLA Modules:
  0.0 320.7 jit_solution(6340486119828184799)
XLA Ops:
  7.4 0.8 compare_select_fusion.1
  9.0 0.9 copy.45
  9.9 0.7 iota_compare_fusion
  10.7 13.1 %gather_fusion = bf16[256,2,2,64,128]{4,3,2,1,0:T(8,128)(2,1)} fusion(bf16[128,2,2,64,128]{4,3,2,1,0:T(8,128)(2,1)} %bitcast.82, s32[1024]{0:T(1024)S(1)} %pad_clamp_fusion.1), kind=kCustom, calls=%fused_computation | custom fusion | bytes 33555456 | tf_op jit(solution)/shard_map/jit(_take)/gather | solution.py:19
  23.8 14.2 %copy_select_fusion = bf16[16,16,2,2,64,128]{5,4,1,3,0,2:T(8,128)(2,1)} fusion(bf16[16,16,2,2,64,128]{5,4,3,2,1,0:T(8,128)(2,1)} %bitcast.81, pred[16,16]{1,0:T(8,128)(4,1)S(1)} %compare_and_fusion), kind=kLoop, calls=%fused_computation.7 | loop fusion | flops 8388608 | bytes 33554688 | tf_op jit(solution)/shard_map/jit(_take)/select_n | solution.py:19
  38.1 8.2 %fusion.36 = (f32[16,2,8,8]{2,3,1,0:T(8,128)S(1)}, f32[16,2,8,8,1032]{4,2,3,1,0:T(8,128)}) fusion(pred[16,8,1032]{2,1,0:T(8,128)(4,1)S(1)} %broadcast_or_fusion, bf16[16,2,2,8,128]{4,3,2,0,1:T(8,128)(2,1)S(1)} %bitcast.89, bf16[16,2,2,1024,128]{4,3,2,0,1:T(8,128)(2,1)} %bitcast.83, bf16[1,1,16,8,16,128]{5,4,3,2,1,0:T(8,128)(2,1)S(1)} %copy-done.3), kind=kOutput, calls=%fused_computation.56 | convolution fusion | flops 566428672 | bytes 26027008 | tf_op jit(solution)/shard_map/sub | solution.py:35
  46.3 7.1 %divide_convert_fusion = bf16[16,2,8,8,1032]{4,2,3,1,0:T(8,128)(2,1)} fusion(f32[16,2,8,8,1032]{4,2,3,1,0:T(8,128)} %get-tuple-element.8, f32[16,2,8,8]{2,3,1,0:T(8,128)S(1)} %get-tuple-element.7), kind=kLoop, calls=%fused_computation.10 | loop fusion | flops 4227072 | bytes 12689408 | tf_op jit(solution)/shard_map/convert_element_type | solution.py:36
  53.5 6.3 %fusion.21 = bf16[16,2,128,8,8]{2,4,3,1,0:T(8,128)(2,1)S(1)} fusion(bf16[16,2,8,8,1032]{4,2,3,1,0:T(8,128)(2,1)} %divide_convert_fusion, bf16[16,2,2,1024,128]{4,3,2,0,1:T(8,128)(2,1)} %bitcast.84, bf16[16,2,2,8,128]{4,3,2,0,1:T(8,128)(2,1)S(1)} %bitcast.90), kind=kOutput, calls=%fused_computation.30 | convolution fusion | flops 558235648 | bytes 21659648 | tf_op jit(solution)/shard_map/rkgwt,rktd->rwkgd/dot_general | solution.py:37
  59.7 1.1 copy.27
  61.0 1.9 gather_fusion.1
  63.1 70.5 %all-gather.2.cloned.1.call-done = bf16[256,8,2048]{2,0,1:T(8,128)(2,1)} async-done(((bf16[16,8,2048]{2,0,1:T(8,128)(2,1)}), bf16[256,8,2048]{2,0,1:T(8,128)(2,1)}) %all-gather.2.cloned.1.call-update) | async-done | bytes 8388624 | tf_op jit(solution)/shard_map/all_gather | solution.py:75
  133.5 8.5 %multiply_reduce_fusion = f32[256,8,64]{0,2,1:T(8,128)S(1)} fusion(bf16[256,8,2048]{2,0,1:T(8,128)(2,1)} %all-gather.2.cloned.1.call-done, bf16[8,64,2048]{2,1,0:T(8,128)(2,1)} %param.20, f32[256,8]{0,1:T(8,128)S(1)} %get-tuple-element.5), kind=kOutput, calls=%fused_computation.27 | convolution fusion | flops 4296933376 | bytes 11018240 | tf_op jit(solution)/shard_map/dot_general | solution.py:85
  142.1 17.1 %all-reduce.1 = bf16[256,8,64]{0,2,1:T(8,128)(2,1)S(1)} all-reduce(f32[256,8,64]{0,2,1:T(8,128)S(1)} %multiply_reduce_fusion), channel_id=1, replica_groups=mesh['section'=2,'tp'=4,'pool'=16] {'tp'}, use_global_device_ids=true, to_apply=%region_4.5 | all-reduce | flops 131072 | bytes 786432 | tf_op jit(solution)/shard_map/psum | solution.py:90
  159.5 2.3 broadcast_multiply_fusion
  161.8 6.5 %mul.56 = bf16[2048,512]{1,0:T(8,128)(2,1)} reshape(bf16[256,8,8,64]{3,2,1,0:T(8,128)(2,1)} %broadcast_multiply_fusion) | data formatting | bytes 4194304 | tf_op jit(solution)/shard_map/mul | solution.py:92
  168.3 8.4 %convolution_convert_fusion = bf16[2048,2048]{1,0:T(8,128)(2,1)} fusion(bf16[2048,512]{1,0:T(8,128)(2,1)} %mul.56, bf16[512,2048]{1,0:T(8,128)(2,1)S(1)} %bitcast.80), kind=kOutput, calls=%fused_computation.22 | convolution fusion | flops 4299161600 | bytes 12582912 | tf_op jit(solution)/shard_map/dot_general | solution.py:96
  176.7 5.3 %all-to-all-start = ((bf16[16,128,2048]{2,1,0:T(8,128)(2,1)}), bf16[16,128,2048]{2,1,0:T(8,128)(2,1)}, u32[]{:S(2)}, u32[]{:S(2)}) async-start(bf16[16,128,2048]{2,1,0:T(8,128)(2,1)} %bitcast.85), calls=%async_computation.1 | async-start | bytes 16777216 | tf_op jit(solution)/shard_map/all_to_all | solution.py:101
  182.0 17.0 %fusion.1 = f32[128,8192]{1,0:T(8,128)} fusion(bf16[128,2048]{1,0:T(8,128)(2,1)S(1)} %bitcast.87, bf16[1,2048,8192]{2,1,0:T(8,128)(2,1)} %param.19), kind=kOutput, calls=%fused_computation.3 | convolution fusion | flops 4294967296 | bytes 38273024 | tf_op jit(solution)/shard_map/dot_general | solution.py:68
  199.1 100.1 %all-to-all-done = bf16[16,128,2048]{2,1,0:T(8,128)(2,1)} async-done(((bf16[16,128,2048]{2,1,0:T(8,128)(2,1)}), bf16[16,128,2048]{2,1,0:T(8,128)(2,1)}, u32[]{:S(2)}, u32[]{:S(2)}) %all-to-all-start) | async-done | bytes 8388640 | tf_op jit(solution)/shard_map/all_to_all | solution.py:101
  299.2 5.3 %convert_reduce_fusion = f32[128,2048]{1,0:T(8,128)S(1)} fusion(bf16[16,128,2048]{2,1,0:T(8,128)(2,1)} %all-to-all-done), kind=kLoop, calls=%fused_computation.8 | loop fusion | flops 8126464 | bytes 9437184 | tf_op jit(solution)/shard_map/reduce_sum | solution.py:104
  304.5 1.5 fusion.27
  306.1 4.9 %collective-permute-start = (bf16[128,2048]{1,0:T(8,128)(2,1)S(1)}, bf16[128,2048]{1,0:T(8,128)(2,1)S(1)}, u32[]{:S(2)}, u32[]{:S(2)}) collective-permute-start(bf16[128,2048]{1,0:T(8,128)(2,1)S(1)} %fusion.27), channel_id=1, source_target_pairs={{0,64},{64,0},{1,65},{65,1},{2,66},{66,2},{3,67},{67,3},{4,68},{68... | collective-permute-start | bytes 1572872 | tf_op jit(solution)/shard_map/ppermute | solution.py:10
  311.0 1.5 collective-permute-done
  312.5 0.8 copy.49
  (27 shorter events, 1.6 us)
Async XLA Ops:
  7.4 160.9 %copy-start = (bf16[8,64,2048]{2,1,0:T(8,128)(2,1)S(1)}, bf16[8,64,2048]{2,1,0:T(8,128)(2,1)}, u32[]{:S(2)}) copy-start(bf16[8,64,2048]{2,1,0:T(8,128)(2,1)} %param.21) | copy-start | bytes 6291460
  7.4 126.2 %all-gather.2.cloned.1.call-start = ((), (), s32[]{:S(2)}) async-start(), calls=%async_computation.3 | async-start | bytes 8912896 | tf_op jit(solution)/shard_map/all_gather | solution.py:75
  23.8 14.3 %copy-start.3 = (bf16[1,1,16,8,16,128]{5,4,3,2,1,0:T(8,128)(2,1)S(1)}, bf16[1,1,16,8,16,128]{5,4,3,2,1,0:T(8,128)(2,1)}, u32[]{:S(2)}) copy-start(bf16[1,1,16,8,16,128]{5,4,3,2,1,0:T(8,128)(2,1)} %param.12) | copy-start | bytes 1572868
  53.5 7.4 %copy-start.2 = (s32[2,16,16]{2,1,0:T(8,128)S(1)}, s32[2,16,16]{2,1,0:T(8,128)}, u32[]{:S(2)}) copy-start(s32[2,16,16]{2,1,0:T(8,128)} %param.17) | copy-start | bytes 6148
  53.5 7.5 %copy-start.1 = (s32[256]{0:T(256)S(1)}, s32[256]{0:T(256)}, u32[]{:S(2)}) copy-start(s32[256]{0:T(256)} %param.18) | copy-start | bytes 3076
  176.7 122.5 %all-to-all-start = ((bf16[16,128,2048]{2,1,0:T(8,128)(2,1)}), bf16[16,128,2048]{2,1,0:T(8,128)(2,1)}, u32[]{:S(2)}, u32[]{:S(2)}) async-start(bf16[16,128,2048]{2,1,0:T(8,128)(2,1)} %bitcast.85), calls=%async_computation.1 | async-start | bytes 16777216 | tf_op jit(solution)/shard_map/all_to_all | solution.py:101
  182.0 122.5 %reduce-scatter.2.cloned.1.call-start = ((), (), s32[]{:S(2)}) async-start(), calls=%async_computation.2 | async-start | bytes 5242880 | tf_op jit(solution)/shard_map/reduce_scatter | solution.py:69
  306.1 6.5 %collective-permute-start = (bf16[128,2048]{1,0:T(8,128)(2,1)S(1)}, bf16[128,2048]{1,0:T(8,128)(2,1)S(1)}, u32[]{:S(2)}, u32[]{:S(2)}) collective-permute-start(bf16[128,2048]{1,0:T(8,128)(2,1)S(1)} %fusion.27), channel_id=1, source_target_pairs={{0,64},{64,0},{1,65},{65,1},{2,66},{66,2},{3,67},{67,3},{4,68},{68... | collective-permute-start | bytes 1572872 | tf_op jit(solution)/shard_map/ppermute | solution.py:10
Sparse Core Ops, SparseCore 0:
  61.0 72.5 all-gather.1
Sparse Core Ops, SparseCore 1:
  199.1 51.5 reduce-scatter.1
where the time goes:
time: 321 us
  waiting for transfers between devices  172 us (54%)
  matrix products  48.3 us (15%)
  other arithmetic  32.9 us (10%)
  local copies, waits for them, and re-layouts  25 us (8%)
  blocking collectives  17.1 us (5%)
  between operations  15 us (5%)
  starting transfers between devices  10.3 us (3%)
    all_to_all x1, waiting for transfers between devices, per_device(): lax.all_to_all(product.astype(jnp.bfloat16), 'pool', split_axis=0, concat...  100 us
    all_gather x1, waiting for transfers between devices, per_device(): everyone = lax.all_gather(context, 'pool', axis=0, tiled=True)  70.5 us
    psum x1, blocking collectives, per_device(): rank_hidden = lax.psum(rank_hidden, 'tp')  17.1 us
    dot_general x1, matrix products, per_device(): partial_out = jnp.dot(flat_rows, wo[0], preferred_element_type=jnp.float32)  17 us
    select_n x2, other arithmetic, attend(): picked = jnp.take(cache_pages, page_rows, axis=0)  15 us
    gather x1, local copies, waits for them, and re-layouts, attend(): picked = jnp.take(cache_pages, page_rows, axis=0)  13.1 us
    dot_general x1, matrix products, per_device(): lax.dot_general(everyone, stacked_down, (((2,), (1,)), ((), ())), preferr...  8.55 us
    dot_general x1, matrix products, per_device(): jnp.dot(broadcast_rows, adapter_up.reshape(pages_per_member * rank_width,...  8.36 us
  transfers between devices with their start and end apart: 4, of which 3 were waited for; matrix products, arithmetic and copies ran while one was open for 8% of the time, Pallas kernels for 0%

commit v1 on v0

--- a/solution.py
+++ b/solution.py
@@ -87,7 +87,11 @@
     )
     wide_rank = wide_rank.reshape(total_requests, window, pages_per_member, rank_width)
     rank_hidden = jnp.sum(wide_rank * owned_mask[:, None, :, None], axis=2)
-    rank_hidden = lax.psum(rank_hidden, "tp")
+    rank_hidden = rank_hidden
+    for hop in (1, 2):
+        rank_hidden = rank_hidden + lax.ppermute(
+            rank_hidden, "tp", [(dev, dev ^ hop) for dev in range(4)]
+        )
     broadcast_rows = (
         rank_hidden.astype(jnp.bfloat16)[:, :, None, :]
         * owned_mask.astype(jnp.bfloat16)[:, None, :, None]

time: 321 us -> 334 us (1.040)
  waiting for transfers between devices: 172 us -> 198 us
  blocking collectives: 17.1 us -> 0 us
    ppermute x0 -> x2, waiting for transfers between devices: none -> 23.9 us  [per_device(): lax.ppermute(rank_hidden, 'tp', [(dev, dev ^ hop) for dev in range(4)])]
    psum x1 -> x0, blocking collectives: 17.1 us -> none  [per_device(): rank_hidden = lax.psum(rank_hidden, 'tp')]
  transfers between devices with their start and end apart: 4 -> 6, of which waited for: 3 -> 5; matrix products, arithmetic and copies ran while one was open for 8% -> 7% of each run, Pallas kernels for 0% -> 0%
where the time goes in v1:
time: 334 us; the launch traced here: 331 us
  waiting for transfers between devices  198 us (59%)
  matrix products  48.3 us (14%)
  other arithmetic  34.1 us (10%)
  local copies, waits for them, and re-layouts  25 us (7%)
  between operations  15 us (4%)
  starting transfers between devices  11.4 us (3%)
    all_to_all x1, waiting for transfers between devices, per_device(): lax.all_to_all(product.astype(jnp.bfloat16), 'pool', split_axis=0, concat...  102 us
    all_gather x1, waiting for transfers between devices, per_device(): everyone = lax.all_gather(context, 'pool', axis=0, tiled=True)  70.6 us
    ppermute x2, waiting for transfers between devices, per_device(): lax.ppermute(rank_hidden, 'tp', [(dev, dev ^ hop) for dev in range(4)])  23.9 us
    dot_general x1, matrix products, per_device(): partial_out = jnp.dot(flat_rows, wo[0], preferred_element_type=jnp.float32)  17 us
    select_n x2, other arithmetic, attend(): picked = jnp.take(cache_pages, page_rows, axis=0)  15 us
    gather x1, local copies, waits for them, and re-layouts, attend(): picked = jnp.take(cache_pages, page_rows, axis=0)  13.1 us
    dot_general x1, matrix products, per_device(): lax.dot_general(everyone, stacked_down, (((2,), (1,)), ((), ())), preferr...  8.55 us
    dot_general x1, matrix products, per_device(): jnp.dot(broadcast_rows, adapter_up.reshape(pages_per_member * rank_width,...  8.3 us
  transfers between devices with their start and end apart: 6, of which 5 were waited for; matrix products, arithmetic and copies ran while one was open for 7% of the time, Pallas kernels for 0%

profile of v1, /device:TPU:35, one launch (start us, length us, event | category | flops | bytes accessed | tf_op | source)
XLA Modules:
  0.0 331.4 jit_solution(17056745631621778246)
XLA Ops:
  9.0 0.9 copy.45
  10.7 13.1 %gather_fusion = bf16[256,2,2,64,128]{4,3,2,1,0:T(8,128)(2,1)} fusion(bf16[128,2,2,64,128]{4,3,2,1,0:T(8,128)(2,1)} %bitcast.82, s32[1024]{0:T(1024)S(1)} %pad_clamp_fusion.1), kind=kCustom, calls=%fused_computation | custom fusion | bytes 33555456 | tf_op jit(solution)/shard_map/jit(_take)/gather | solution.py:19
  23.8 14.2 %copy_select_fusion = bf16[16,16,2,2,64,128]{5,4,1,3,0,2:T(8,128)(2,1)} fusion(bf16[16,16,2,2,64,128]{5,4,3,2,1,0:T(8,128)(2,1)} %bitcast.81, pred[16,16]{1,0:T(8,128)(4,1)S(1)} %compare_and_fusion), kind=kLoop, calls=%fused_computation.7 | loop fusion | flops 8388608 | bytes 33554688 | tf_op jit(solution)/shard_map/jit(_take)/select_n | solution.py:19
  38.1 8.2 %fusion.36 = (f32[16,2,8,8]{2,3,1,0:T(8,128)S(1)}, f32[16,2,8,8,1032]{4,2,3,1,0:T(8,128)}) fusion(pred[16,8,1032]{2,1,0:T(8,128)(4,1)S(1)} %broadcast_or_fusion, bf16[16,2,2,8,128]{4,3,2,0,1:T(8,128)(2,1)S(1)} %bitcast.89, bf16[16,2,2,1024,128]{4,3,2,0,1:T(8,128)(2,1)} %bitcast.83, bf16[1,1,16,8,16,128]{5,4,3,2,1,0:T(8,128)(2,1)S(1)} %copy-done.3), kind=kOutput, calls=%fused_computation.57 | convolution fusion | flops 566428672 | bytes 26027008 | tf_op jit(solution)/shard_map/sub | solution.py:35
  46.3 7.1 %divide_convert_fusion = bf16[16,2,8,8,1032]{4,2,3,1,0:T(8,128)(2,1)} fusion(f32[16,2,8,8,1032]{4,2,3,1,0:T(8,128)} %get-tuple-element.8, f32[16,2,8,8]{2,3,1,0:T(8,128)S(1)} %get-tuple-element.7), kind=kLoop, calls=%fused_computation.10 | loop fusion | flops 4227072 | bytes 12689408 | tf_op jit(solution)/shard_map/convert_element_type | solution.py:36
  53.5 6.3 %fusion.21 = bf16[16,2,128,8,8]{2,4,3,1,0:T(8,128)(2,1)S(1)} fusion(bf16[16,2,8,8,1032]{4,2,3,1,0:T(8,128)(2,1)} %divide_convert_fusion, bf16[16,2,2,1024,128]{4,3,2,0,1:T(8,128)(2,1)} %bitcast.84, bf16[16,2,2,8,128]{4,3,2,0,1:T(8,128)(2,1)S(1)} %bitcast.90), kind=kOutput, calls=%fused_computation.30 | convolution fusion | flops 558235648 | bytes 21659648 | tf_op jit(solution)/shard_map/rkgwt,rktd->rwkgd/dot_general | solution.py:37
  59.7 1.1 copy.27
  61.0 1.9 gather_fusion.1
  63.0 70.6 %all-gather.2.cloned.1.call-done = bf16[256,8,2048]{2,0,1:T(8,128)(2,1)} async-done(((bf16[16,8,2048]{2,0,1:T(8,128)(2,1)}), bf16[256,8,2048]{2,0,1:T(8,128)(2,1)}) %all-gather.2.cloned.1.call-update) | async-done | bytes 8388624 | tf_op jit(solution)/shard_map/all_gather | solution.py:75
  133.5 8.5 %multiply_reduce_fusion = f32[256,8,64]{0,2,1:T(8,128)S(1)} fusion(bf16[256,8,2048]{2,0,1:T(8,128)(2,1)} %all-gather.2.cloned.1.call-done, bf16[8,64,2048]{2,1,0:T(8,128)(2,1)} %param.20, f32[256,8]{0,1:T(8,128)S(1)} %get-tuple-element.5), kind=kOutput, calls=%fused_computation.27 | convolution fusion | flops 4296933376 | bytes 11018240 | tf_op jit(solution)/shard_map/dot_general | solution.py:85
  142.5 12.4 %collective-permute-done = f32[256,8,64]{0,2,1:T(8,128)S(1)} collective-permute-done((f32[256,8,64]{0,2,1:T(8,128)S(1)}, f32[256,8,64]{0,2,1:T(8,128)S(1)}, u32[]{:S(2)}, u32[]{:S(2)}) %collective-permute-start) | collective-permute-done | bytes 524320 | tf_op jit(solution)/shard_map/ppermute | solution.py:92
  154.9 2.0 collective-permute-start.1
  157.1 11.5 %collective-permute-done.1 = f32[256,8,64]{0,2,1:T(8,128)} collective-permute-done((f32[256,8,64]{0,2,1:T(8,128)S(1)}, f32[256,8,64]{0,2,1:T(8,128)}, u32[]{:S(2)}, u32[]{:S(2)}) %collective-permute-start.1) | collective-permute-done | bytes 524320 | tf_op jit(solution)/shard_map/ppermute | solution.py:92
  168.6 1.1 add_convert_fusion
  170.0 2.3 broadcast_multiply_fusion
  172.3 6.5 %mul.56 = bf16[2048,512]{1,0:T(8,128)(2,1)} reshape(bf16[256,8,8,64]{3,2,1,0:T(8,128)(2,1)} %broadcast_multiply_fusion) | data formatting | bytes 4194304 | tf_op jit(solution)/shard_map/mul | solution.py:96
  178.8 8.3 %convolution_convert_fusion = bf16[2048,2048]{1,0:T(8,128)(2,1)} fusion(bf16[2048,512]{1,0:T(8,128)(2,1)} %mul.56, bf16[512,2048]{1,0:T(8,128)(2,1)S(1)} %bitcast.80), kind=kOutput, calls=%fused_computation.22 | convolution fusion | flops 4299161600 | bytes 12582912 | tf_op jit(solution)/shard_map/dot_general | solution.py:100
  187.1 5.3 %all-to-all-start = ((bf16[16,128,2048]{2,1,0:T(8,128)(2,1)}), bf16[16,128,2048]{2,1,0:T(8,128)(2,1)}, u32[]{:S(2)}, u32[]{:S(2)}) async-start(bf16[16,128,2048]{2,1,0:T(8,128)(2,1)} %bitcast.85), calls=%async_computation.1 | async-start | bytes 16777216 | tf_op jit(solution)/shard_map/all_to_all | solution.py:105
  192.4 17.0 %fusion.1 = f32[128,8192]{1,0:T(8,128)} fusion(bf16[128,2048]{1,0:T(8,128)(2,1)S(1)} %bitcast.87, bf16[1,2048,8192]{2,1,0:T(8,128)(2,1)} %param.19), kind=kOutput, calls=%fused_computation.3 | convolution fusion | flops 4294967296 | bytes 38273024 | tf_op jit(solution)/shard_map/dot_general | solution.py:68
  209.5 101.6 %all-to-all-done = bf16[16,128,2048]{2,1,0:T(8,128)(2,1)} async-done(((bf16[16,128,2048]{2,1,0:T(8,128)(2,1)}), bf16[16,128,2048]{2,1,0:T(8,128)(2,1)}, u32[]{:S(2)}, u32[]{:S(2)}) %all-to-all-start) | async-done | bytes 8388640 | tf_op jit(solution)/shard_map/all_to_all | solution.py:105
  311.1 5.3 %convert_reduce_fusion = f32[128,2048]{1,0:T(8,128)S(1)} fusion(bf16[16,128,2048]{2,1,0:T(8,128)(2,1)} %all-to-all-done), kind=kLoop, calls=%fused_computation.8 | loop fusion | flops 8126464 | bytes 9437184 | tf_op jit(solution)/shard_map/reduce_sum | solution.py:108
  316.4 1.5 fusion.27
  317.9 3.7 %collective-permute-start.2 = (bf16[128,2048]{1,0:T(8,128)(2,1)S(1)}, bf16[128,2048]{1,0:T(8,128)(2,1)S(1)}, u32[]{:S(2)}, u32[]{:S(2)}) collective-permute-start(bf16[128,2048]{1,0:T(8,128)(2,1)S(1)} %fusion.27), channel_id=1, source_target_pairs={{0,64},{64,0},{1,65},{65,1},{2,66},{66,2},{3,67},{67,3},{4,68},{68... | collective-permute-start | bytes 1572872 | tf_op jit(solution)/shard_map/ppermute | solution.py:10
  321.6 1.5 collective-permute-done.2
  (32 shorter events, 4.4 us)
Async XLA Ops:
  7.4 171.4 %copy-start = (bf16[8,64,2048]{2,1,0:T(8,128)(2,1)S(1)}, bf16[8,64,2048]{2,1,0:T(8,128)(2,1)}, u32[]{:S(2)}) copy-start(bf16[8,64,2048]{2,1,0:T(8,128)(2,1)} %param.21) | copy-start | bytes 6291460
  7.4 126.2 %all-gather.2.cloned.1.call-start = ((), (), s32[]{:S(2)}) async-start(), calls=%async_computation.3 | async-start | bytes 8912896 | tf_op jit(solution)/shard_map/all_gather | solution.py:75
  23.8 14.3 %copy-start.3 = (bf16[1,1,16,8,16,128]{5,4,3,2,1,0:T(8,128)(2,1)S(1)}, bf16[1,1,16,8,16,128]{5,4,3,2,1,0:T(8,128)(2,1)}, u32[]{:S(2)}) copy-start(bf16[1,1,16,8,16,128]{5,4,3,2,1,0:T(8,128)(2,1)} %param.12) | copy-start | bytes 1572868
  53.5 7.4 %copy-start.2 = (s32[2,16,16]{2,1,0:T(8,128)S(1)}, s32[2,16,16]{2,1,0:T(8,128)}, u32[]{:S(2)}) copy-start(s32[2,16,16]{2,1,0:T(8,128)} %param.17) | copy-start | bytes 6148
  53.5 7.5 %copy-start.1 = (s32[256]{0:T(256)S(1)}, s32[256]{0:T(256)}, u32[]{:S(2)}) copy-start(s32[256]{0:T(256)} %param.18) | copy-start | bytes 3076
  142.1 12.7 %collective-permute-start = (f32[256,8,64]{0,2,1:T(8,128)S(1)}, f32[256,8,64]{0,2,1:T(8,128)S(1)}, u32[]{:S(2)}, u32[]{:S(2)}) collective-permute-start(f32[256,8,64]{0,2,1:T(8,128)S(1)} %multiply_reduce_fusion), channel_id=1, source_target_pairs={{0,16},{16,0},{32,48},{48,32},{1,17},{17,1},{33,49},{49,33},{2,18}... | collective-permute-start | bytes 1572872 | tf_op jit(solution)/shard_map/ppermute | solution.py:92
  154.9 13.7 %collective-permute-start.1 = (f32[256,8,64]{0,2,1:T(8,128)S(1)}, f32[256,8,64]{0,2,1:T(8,128)}, u32[]{:S(2)}, u32[]{:S(2)}) collective-permute-start(f32[256,8,64]{0,2,1:T(8,128)S(1)} %add.84), channel_id=1, source_target_pairs={{0,32},{16,48},{32,0},{48,16},{1,33},{17,49},{33,1},{49,17},{2,34}... | collective-permute-start | bytes 1572872 | tf_op jit(solution)/shard_map/ppermute | solution.py:92
  187.1 124.0 %all-to-all-start = ((bf16[16,128,2048]{2,1,0:T(8,128)(2,1)}), bf16[16,128,2048]{2,1,0:T(8,128)(2,1)}, u32[]{:S(2)}, u32[]{:S(2)}) async-start(bf16[16,128,2048]{2,1,0:T(8,128)(2,1)} %bitcast.85), calls=%async_computation.1 | async-start | bytes 16777216 | tf_op jit(solution)/shard_map/all_to_all | solution.py:105
  192.4 124.0 %reduce-scatter.2.cloned.1.call-start = ((), (), s32[]{:S(2)}) async-start(), calls=%async_computation.2 | async-start | bytes 5242880 | tf_op jit(solution)/shard_map/reduce_scatter | solution.py:69
  317.9 5.2 %collective-permute-start.2 = (bf16[128,2048]{1,0:T(8,128)(2,1)S(1)}, bf16[128,2048]{1,0:T(8,128)(2,1)S(1)}, u32[]{:S(2)}, u32[]{:S(2)}) collective-permute-start(bf16[128,2048]{1,0:T(8,128)(2,1)S(1)} %fusion.27), channel_id=1, source_target_pairs={{0,64},{64,0},{1,65},{65,1},{2,66},{66,2},{3,67},{67,3},{4,68},{68... | collective-permute-start | bytes 1572872 | tf_op jit(solution)/shard_map/ppermute | solution.py:10
Sparse Core Ops, SparseCore 0:
  61.0 72.5 all-gather.1
Sparse Core Ops, SparseCore 1:
  209.6 48.9 reduce-scatter.1
